TPU v7x, 32 devices: a whole 2x2x4 slice. The times are simulated.
32 devices in a mesh: ka: 4 (over y, core), op: 4 (over z), row: 2 (over x).
Axes of the slice: x: 2, y: 2, z: 4, core: 2. Of those that a mesh axis runs over, the one named last changes fastest.
Arguments:
- kgrid: int32 [3, 256], P(None, ('ka', 'op', 'row')), may hold values from 0 to 63
- rvec: int32 [3, 256], replicated, may hold values from -8 to 8
- degen: int32 [256], replicated, may hold values from 1 to 4
- operators: bfloat16 [4, 256, 12800], P('op', ('ka', 'row')), may hold values from -1 to 1
- vectors: bfloat16 [256, 12800], P(('ka', 'op', 'row')), may hold values from -0.5 to 0.5
Outputs:
- density: float32 [3, 256], P(None, ('ka', 'op', 'row'))
- magnetization: float32 [3], replicated
All inputs are finite; a program needn't handle non-finite values.
Results may differ from a plain program's by a relative error of at most 0.012.
Values may be sent and summed in bfloat16 or wider, within the bound.
No kernel may reach another device: no remote copies, remote signals or barrier semaphores. Data moves between devices by JAX's collectives and lax.ppermute only.
A program may use at most 64 MiB of HBM per device.

v0:
```python
import math
import jax
import jax.numpy as jnp
from jax import lax
from jax.sharding import PartitionSpec as P

W = 80
GRID = 64
SMEARING = 0.5


def phase_pair(points, lattice, weights):
    winding = (
        points[0][:, None] * lattice[0][None, :]
        + points[1][:, None] * lattice[1][None, :]
        + points[2][:, None] * lattice[2][None, :]
    )
    winding = jnp.mod(winding, GRID)
    angle = 2.0 * math.pi / GRID * winding.astype(jnp.float32)
    inverse = 1.0 / weights.astype(jnp.float32)
    cosine = (jnp.cos(angle) * inverse[None, :]).astype(jnp.bfloat16)
    sine = (jnp.sin(angle) * inverse[None, :]).astype(jnp.bfloat16)
    return (cosine, sine)


def mix_table(table, block):
    return jnp.einsum("kr,nrx->nkx", table, block, preferred_element_type=jnp.float32)


def make_fold(points, lattice, weights):

    def accumulate(carry, piece, start):
        cosine, sine = phase_pair(points, lattice, weights)
        half = piece.shape[2] // 2
        real_in = piece[:, :, :half]
        imag_in = piece[:, :, half:]
        real_out = mix_table(cosine, real_in) - mix_table(sine, imag_in)
        imag_out = mix_table(cosine, imag_in) + mix_table(sine, real_in)
        return jnp.concatenate([real_out, imag_out], axis=1)

    return accumulate


def density_terms(rot_real, rot_imag):
    ham_real = rot_real[0]
    ham_imag = rot_imag[0]
    conn_real = rot_real[1:]
    conn_imag = rot_imag[1:]
    levels = jnp.diagonal(ham_real, axis1=1, axis2=2).astype(jnp.float32)
    filled = jax.nn.sigmoid(-levels / SMEARING)
    vacant = 1.0 - filled

    def multiply(left, right):
        return jnp.einsum("knm,bkml->bknl", left, right, preferred_element_type=jnp.float32)

    prod_real = multiply(ham_real, conn_real) - multiply(ham_imag, conn_imag)
    prod_imag = multiply(ham_real, conn_imag) + multiply(ham_imag, conn_real)
    weight = filled[None, :, :, None] * vacant[None, :, None, :]
    left_real = conn_real.astype(jnp.float32) * weight
    left_imag = conn_imag.astype(jnp.float32) * weight
    traces = jnp.einsum(
        "aknm,bkmn->abk", left_real, prod_imag, precision=lax.Precision.HIGHEST
    ) + jnp.einsum("aknm,bkmn->abk", left_imag, prod_real, precision=lax.Precision.HIGHEST)
    density = jnp.stack(
        [traces[1, 2] - traces[2, 1], traces[2, 0] - traces[0, 2], traces[0, 1] - traces[1, 0]]
    )
    return density / W


def per_device(kgrid, rvec, degen, operators, vectors):
    own = kgrid.shape[1]
    entries = vectors.shape[1] // 2
    count_ka = lax.axis_size("ka")
    count_op = lax.axis_size("op")
    count_row = lax.axis_size("row")
    count_all = own * count_ka * count_op * count_row
    points = lax.all_gather(kgrid, "op", axis=1, tiled=True)
    folder = make_fold(points, rvec, degen)
    points_count = points.shape[1]
    zeroed = jnp.zeros((1, 2 * points_count, entries), jnp.float32)
    summed = folder(
        zeroed, lax.all_gather(operators, ("ka", "row"), axis=1, tiled=True), jnp.int32(0)
    )
    real_k = summed[:, :points_count].astype(jnp.bfloat16)
    imag_k = summed[:, points_count:].astype(jnp.bfloat16)
    real_k, imag_k = (
        lax.all_to_all(real_k, "op", split_axis=1, concat_axis=0, tiled=True),
        lax.all_to_all(imag_k, "op", split_axis=1, concat_axis=0, tiled=True),
    )
    halves = vectors.reshape(own, 2, W, W)
    vec_real = halves[:, 0]
    vec_imag = halves[:, 1]

    def apply_right(left, right):
        return jnp.einsum("kij,kjn->kin", left, right, preferred_element_type=jnp.float32)

    def apply_left(left, right):
        return jnp.einsum("kin,kim->knm", left, right, preferred_element_type=jnp.float32)

    def rotate(block):
        op_real, op_imag = block
        prod_real = (apply_right(op_real, vec_real) - apply_right(op_imag, vec_imag)).astype(
            jnp.bfloat16
        )
        prod_imag = (apply_right(op_real, vec_imag) + apply_right(op_imag, vec_real)).astype(
            jnp.bfloat16
        )
        rot_real = (apply_left(vec_real, prod_real) + apply_left(vec_imag, prod_imag)).astype(
            jnp.bfloat16
        )
        rot_imag = (apply_left(vec_real, prod_imag) - apply_left(vec_imag, prod_real)).astype(
            jnp.bfloat16
        )
        return (rot_real, rot_imag)

    rot_real, rot_imag = lax.map(
        rotate, (real_k.reshape(4, own, W, W), imag_k.reshape(4, own, W, W))
    )
    density = density_terms(rot_real, rot_imag)
    magnetization = lax.psum(jnp.sum(density, axis=1), ("ka", "op", "row")) / count_all
    return (density, magnetization)


def solution(mesh):
    in_specs = (
        P(None, ("ka", "op", "row")),
        P(),
        P(),
        P("op", ("ka", "row"), None),
        P(("ka", "op", "row"), None),
    )
    out_specs = (P(None, ("ka", "op", "row")), P())
    return jax.shard_map(
        per_device, mesh=mesh, in_specs=in_specs, out_specs=out_specs, check_vma=False
    )
```

profile of v0, /device:TPU:10, one launch (start us, length us, event | category | flops | bytes accessed | tf_op | source)
XLA Modules:
  0.0 192.2 jit_solution(1296548206554515161)
XLA Ops:
  7.9 12.3 %all-gather = s32[4,8,3]{1,2,0:T(4,128)S(1)} all-gather(s32[1,8,3]{1,2,0:T(4,128)} %bitcast.177), channel_id=1, replica_groups=mesh['ka'=4,'op'=4,'row'=2] {'op'}, dimensions={0}, use_global_device_ids=true | all-gather | bytes 480 | tf_op jit(solution)/shard_map/all_gather | solution.py:77
  21.8 35.7 %all-gather.3.cloned.1.call-done = bf16[1,256,12800]{2,1,0:T(8,128)(2,1)} async-done(((bf16[1,32,12800]{2,1,0:T(8,128)(2,1)}), bf16[1,256,12800]{2,1,0:T(8,128)(2,1)}) %all-gather.3.cloned.1.call-update) | async-done | bytes 6553616 | tf_op jit(solution)/shard_map/all_gather | solution.py:82
  57.5 2.8 %fusion.26 = f32[32,6400]{1,0:T(8,128)S(1)} fusion(bf16[1,256,12800]{2,1,0:T(8,128)(2,1)} %all-gather.3.cloned.1.call-done, f32[256]{0:T(256)S(1)} %convert_divide_fusion, s32[256]{0:T(256)S(1)} %bitcast.168, s32[32]{0:T(128)S(1)} %get-tuple-element.69, s32[256]{0:T(256)S(1)} %bitcast.172, s32[32]{0:T(128)S(1)} %get-tuple-element.70, s32[256]{0:T(256)S(1)} %bitcast.164, ...), kind=kOutput, calls=%fused_computation.35 | convolution fusion | flops 105021440 | bytes 4100480 | tf_op jit(solution)/shard_map/kr,nrx->nkx/dot_general | solution.py:27
  60.3 2.8 %fusion.25 = bf16[1,32,6400]{2,1,0:T(8,128)(2,1)S(1)} fusion(f32[32,6400]{1,0:T(8,128)S(1)} %fusion.26, bf16[1,256,12800]{2,1,0:T(8,128)(2,1)} %all-gather.3.cloned.1.call-done, f32[256]{0:T(256)S(1)} %convert_divide_fusion, s32[256]{0:T(256)S(1)} %bitcast.169, s32[32]{0:T(128)S(1)} %get-tuple-element.69, s32[256]{0:T(256)S(1)} %bitcast.173, ...), kind=kOutput, calls=%fused_computation.32 | convolution fusion | flops 105431040 | bytes 4510080 | tf_op jit(solution)/shard_map/kr,nrx->nkx/dot_general | solution.py:27
  64.2 3.1 %reduce.10 = bf16[32,6400]{1,0:T(8,128)(2,1)S(1)} reduce(bf16[32,1,6400]{2,1,0:T(2,128)(2,1)S(1)} %bitcast.162, bf16[]{:T(256)} %broadcast.118), dimensions={1}, to_apply=%bitcast.125.reduce_sub_computation | reduce | bytes 819202
  68.2 5.1 %all-to-all-start = ((bf16[4,2,25600]{2,1,0:T(2,128)(2,1)}), bf16[4,2,25600]{2,1,0:T(2,128)(2,1)S(1)}, u32[]{:S(2)}, u32[]{:S(2)}) async-start(bf16[4,2,25600]{2,1,0:T(2,128)(2,1)} %reshape.142), calls=%async_computation | async-start | bytes 819200 | tf_op jit(solution)/shard_map/all_to_all | solution.py:87
  73.3 2.8 %fusion.27 = f32[32,6400]{1,0:T(8,128)S(1)} fusion(bf16[1,256,12800]{2,1,0:T(8,128)(2,1)} %all-gather.3.cloned.1.call-done, f32[256]{0:T(256)S(1)} %convert_divide_fusion, s32[256]{0:T(256)S(1)} %bitcast.170, s32[32]{0:T(128)S(1)} %get-tuple-element.69, s32[256]{0:T(256)S(1)} %bitcast.174, s32[32]{0:T(128)S(1)} %get-tuple-element.70, s32[256]{0:T(256)S(1)} %bitcast.166, ...), kind=kOutput, calls=%fused_computation.36 | convolution fusion | flops 105021440 | bytes 4100480 | tf_op jit(solution)/shard_map/kr,nrx->nkx/dot_general | solution.py:27
  76.1 2.8 %fusion.24 = bf16[1,32,6400]{2,1,0:T(8,128)(2,1)S(1)} fusion(f32[32,6400]{1,0:T(8,128)S(1)} %fusion.27, bf16[1,256,12800]{2,1,0:T(8,128)(2,1)} %all-gather.3.cloned.1.call-done, f32[256]{0:T(256)S(1)} %convert_divide_fusion, s32[256]{0:T(256)S(1)} %bitcast.171, s32[32]{0:T(128)S(1)} %get-tuple-element.69, s32[256]{0:T(256)S(1)} %bitcast.175, ...), kind=kOutput, calls=%fused_computation.31 | convolution fusion | flops 105431040 | bytes 4510080 | tf_op jit(solution)/shard_map/kr,nrx->nkx/dot_general | solution.py:27
  79.6 3.1 %reduce.11 = bf16[32,6400]{1,0:T(8,128)(2,1)S(1)} reduce(bf16[32,1,6400]{2,1,0:T(2,128)(2,1)S(1)} %bitcast.163, bf16[]{:T(256)} %broadcast.118), dimensions={1}, to_apply=%bitcast.124.reduce_sub_computation | reduce | bytes 819202
  83.5 5.7 %all-to-all-start.1 = ((bf16[4,2,25600]{2,1,0:T(2,128)(2,1)}), bf16[4,2,25600]{2,1,0:T(2,128)(2,1)S(1)}, u32[]{:S(2)}, u32[]{:S(2)}) async-start(bf16[4,2,25600]{2,1,0:T(2,128)(2,1)} %reshape.144), calls=%async_computation.1 | async-start | bytes 819200 | tf_op jit(solution)/shard_map/all_to_all | solution.py:88
  90.1 2.3 %bitcast_reduce_fusion.1 = bf16[32,6400]{1,0:T(8,128)(2,1)S(1)} fusion(bf16[32,1,6400]{2,1,0:T(2,128)(2,1)S(1)} %reshape.143), kind=kLoop, calls=%fused_computation.108 | loop fusion | bytes 819200 | tf_op jit(solution)/shard_map/all_to_all | solution.py:87
  93.4 4.8 %all-to-all-done.1 = bf16[4,2,25600]{2,1,0:T(2,128)(2,1)S(1)} async-done(((bf16[4,2,25600]{2,1,0:T(2,128)(2,1)}), bf16[4,2,25600]{2,1,0:T(2,128)(2,1)S(1)}, u32[]{:S(2)}, u32[]{:S(2)}) %all-to-all-start.1) | async-done | bytes 409632 | tf_op jit(solution)/shard_map/all_to_all | solution.py:88
  98.6 2.3 %bitcast_reduce_fusion = bf16[32,6400]{1,0:T(8,128)(2,1)S(1)} fusion(bf16[32,1,6400]{2,1,0:T(2,128)(2,1)S(1)} %reshape.145), kind=kLoop, calls=%fused_computation.107 | loop fusion | bytes 819200 | tf_op jit(solution)/shard_map/all_to_all | solution.py:88
  102.0 7.9 %while.12 = (s32[]{:T(128)}, bf16[4,8,80,80]{2,3,1,0:T(8,128)(2,1)S(1)}, bf16[4,8,80,80]{2,3,1,0:T(8,128)(2,1)S(1)}, bf16[4,8,80,80]{3,2,1,0:T(8,128)(2,1)S(1)},...) while((s32[]{:T(128)}, ...), condition=%wide.region_1.2_spmd, body=%wide.region_0.1_spmd.sunk | while | flops 65945600 | bytes 5038189 | solution.py:116
  110.5 1.6 copy.74
  112.1 3.7 %gather_fusion = bf16[80,8]{1,0:T(8,128)(2,1)S(1)} fusion(bf16[8,80,80]{0,2,1:T(8,128)(2,1)} %copy.74, s32[80]{0:T(128)S(1)} %or_bitcast_fusion), kind=kCustom, calls=%fused_computation | custom fusion | bytes 3200 | tf_op jit(solution)/shard_map/jit(diagonal)/gather | solution.py:49
  117.0 1.2 fusion.48
  118.2 2.2 %fusion.28 = f32[3,8,80,80]{2,3,0,1:T(8,128)} fusion(f32[8,3,80,80]{3,2,1,0:T(8,128)S(1)} %fusion.46, bf16[4,8,80,80]{3,2,1,0:T(8,128)(2,1)} %copy.73, bf16[4,8,80,80]{2,3,1,0:T(8,128)(2,1)S(1)} %get-tuple-element.40), kind=kOutput, calls=%fused_computation.38 | convolution fusion | flops 24729600 | bytes 1802240 | tf_op jit(solution)/shard_map/knm,bkml->bknl/dot_general | solution.py:54
  120.4 2.4 %copy.78 = f32[3,8,80,80]{3,0,2,1:T(4,128)} copy(f32[3,8,80,80]{2,3,0,1:T(8,128)} %fusion.28) | data formatting | bytes 1228800 | tf_op jit(solution)/shard_map/sub | solution.py:56
  124.1 2.1 %fusion.29 = f32[3,8,80,80]{2,3,0,1:T(8,128)} fusion(f32[8,3,80,80]{3,2,1,0:T(8,128)S(1)} %fusion.48, bf16[4,8,80,80]{3,2,1,0:T(8,128)(2,1)} %copy.73, bf16[4,8,80,80]{2,3,1,0:T(8,128)(2,1)S(1)} %get-tuple-element.41), kind=kOutput, calls=%fused_computation.40 | convolution fusion | flops 24729600 | bytes 1802240 | tf_op jit(solution)/shard_map/knm,bkml->bknl/dot_general | solution.py:54
  126.2 2.4 %copy.76 = f32[3,8,80,80]{3,0,2,1:T(4,128)} copy(f32[3,8,80,80]{2,3,0,1:T(8,128)} %fusion.29) | data formatting | bytes 1228800 | tf_op jit(solution)/shard_map/add | solution.py:57
  128.7 7.4 %fusion.34 = f32[8,3,3]{2,1,0:T(4,128)S(1)} fusion(f32[3,8,80,80]{3,0,2,1:T(4,128)} %copy.76, f32[3,8,80,80]{2,3,0,1:T(8,128)S(1)} %get-tuple-element.62), kind=kOutput, calls=%fused_computation.45 | convolution fusion | flops 5529600 | bytes 1229088 | tf_op jit(solution)/shard_map/aknm,bkmn->abk/dot_general | solution.py:61
  136.0 6.8 %fusion.43 = f32[3,3,8]{0,1,2:T(4,128)S(1)} fusion(f32[8,3,3]{2,1,0:T(4,128)S(1)} %fusion.34, f32[3,8,80,80]{3,0,2,1:T(4,128)} %copy.78, f32[3,8,80,80]{2,3,0,1:T(8,128)S(1)} %copy-done), kind=kOutput, calls=%fused_computation.48 | convolution fusion | flops 5529672 | bytes 1229376 | tf_op jit(solution)/shard_map/aknm,bkmn->abk/dot_general | solution.py:63
  143.7 41.1 %psum.7 = f32[3]{0:T(128)S(1)} all-reduce(f32[3]{0:T(128)S(1)} %get-tuple-element.59), channel_id=1, replica_groups=mesh['ka'=4,'op'=4,'row'=2] {'ka','op','row'}, use_global_device_ids=true, to_apply=%region_3.4 | all-reduce | flops 3 | bytes 24 | tf_op jit(solution)/shard_map/psum | solution.py:120
  (72 shorter events, 21.4 us)
Async XLA Ops:
  7.2 50.4 %all-gather.3.cloned.1.call-start = ((), (), s32[]{:S(2)}) async-start(), calls=%async_computation.2 | async-start | bytes 7372800 | tf_op jit(solution)/shard_map/all_gather | solution.py:82
  68.2 15.3 %all-to-all-start = ((bf16[4,2,25600]{2,1,0:T(2,128)(2,1)}), bf16[4,2,25600]{2,1,0:T(2,128)(2,1)S(1)}, u32[]{:S(2)}, u32[]{:S(2)}) async-start(bf16[4,2,25600]{2,1,0:T(2,128)(2,1)} %reshape.142), calls=%async_computation | async-start | bytes 819200 | tf_op jit(solution)/shard_map/all_to_all | solution.py:87
  76.1 13.1 %copy-start.2 = (bf16[8,12800]{1,0:T(8,128)(2,1)S(1)}, bf16[8,12800]{1,0:T(8,128)(2,1)}, u32[]{:S(2)}) copy-start(bf16[8,12800]{1,0:T(8,128)(2,1)} %param.11) | copy-start | bytes 614404
  83.5 14.7 %all-to-all-start.1 = ((bf16[4,2,25600]{2,1,0:T(2,128)(2,1)}), bf16[4,2,25600]{2,1,0:T(2,128)(2,1)S(1)}, u32[]{:S(2)}, u32[]{:S(2)}) async-start(bf16[4,2,25600]{2,1,0:T(2,128)(2,1)} %reshape.144), calls=%async_computation.1 | async-start | bytes 819200 | tf_op jit(solution)/shard_map/all_to_all | solution.py:88
  110.2 5.7 %copy-start.1 = (bf16[4,8,80,80]{3,2,1,0:T(8,128)(2,1)}, bf16[4,8,80,80]{3,2,1,0:T(8,128)(2,1)S(1)}, u32[]{:S(2)}) copy-start(bf16[4,8,80,80]{3,2,1,0:T(8,128)(2,1)S(1)} %copy.71) | copy-start | bytes 1228804
  126.2 9.8 %copy-start = (f32[3,8,80,80]{2,3,0,1:T(8,128)S(1)}, f32[3,8,80,80]{2,3,0,1:T(8,128)}, u32[]{:S(2)}) copy-start(f32[3,8,80,80]{2,3,0,1:T(8,128)} %get-tuple-element.61) | copy-start | bytes 1843204
Sparse Core Ops, SparseCore 0:
  9.9 47.6 all-gather.2
where the time goes:
time: 193 us; the launch traced here: 192 us
  blocking collectives  53.4 us (28%)
  waiting for transfers between devices  41.2 us (21%)
  matrix products  38.6 us (20%)
  local copies, waits for them, and re-layouts  24 us (12%)
  between operations  14.2 us (7%)
  starting transfers between devices  10.9 us (6%)
  other arithmetic  9.58 us (5%)
    psum x1, blocking collectives, per_device(): lax.psum(jnp.sum(density, axis=1), ('ka', 'op', 'row')) / count_all  41.1 us
    all_gather x1, waiting for transfers between devices, per_device(): lax.all_gather(operators, ('ka', 'row'), axis=1, tiled=True)  35.7 us
    all_gather x1, blocking collectives, per_device(): points = lax.all_gather(kgrid, 'op', axis=1, tiled=True)  12.3 us
    dot_general x4, matrix products, mix_table(): jnp.einsum('kr,nrx->nkx', table, block, preferred_element_type=jnp.float32)  11.1 us
    dot_general x1, matrix products, density_terms(): jnp.einsum('aknm,bkmn->abk', left_real, prod_imag, precision=lax.Precisio...  7.35 us
    dot_general x1, matrix products, density_terms(): jnp.einsum('aknm,bkmn->abk', left_imag, prod_real, precision=lax.Precisio...  6.79 us
    unnamed x2, other arithmetic  6.14 us
    dot_general x4, matrix products, multiply(): jnp.einsum('knm,bkml->bknl', left, right, preferred_element_type=jnp.floa...  5.81 us
  transfers between devices with their start and end apart: 3, of which 2 were waited for; matrix products, arithmetic and copies ran while one was open for 8% of the time, Pallas kernels for 0%

commit v1 on v0

--- a/solution.py
+++ b/solution.py
@@ -117,7 +117,7 @@
         rotate, (real_k.reshape(4, own, W, W), imag_k.reshape(4, own, W, W))
     )
     density = density_terms(rot_real, rot_imag)
-    magnetization = lax.psum(jnp.sum(density, axis=1), ("ka", "op", "row")) / count_all
+    magnetization = lax.psum(lax.psum(jnp.sum(density, axis=1), ("op", "row")), "ka") / count_all
     return (density, magnetization)
 
 

time: 193 us -> 181 us (0.938)
  the two profiles are of different devices: /device:TPU:10 before, /device:TPU:0 now
where the time goes in v1:
time: 181 us; the launch traced here: 180 us
  waiting for transfers between devices  45.9 us (25%)
  blocking collectives  39.2 us (22%)
  matrix products  38.7 us (21%)
  local copies, waits for them, and re-layouts  24 us (13%)
  between operations  14.2 us (8%)
  other arithmetic  9.58 us (5%)
  starting transfers between devices  8.28 us (5%)
    all_gather x1, waiting for transfers between devices, per_device(): lax.all_gather(operators, ('ka', 'row'), axis=1, tiled=True)  35.9 us
    psum x1, blocking collectives, per_device(): lax.psum(jnp.sum(density, axis=1), ('op', 'row'))  19.5 us
    all_gather x1, blocking collectives, per_device(): points = lax.all_gather(kgrid, 'op', axis=1, tiled=True)  13.8 us
    dot_general x4, matrix products, mix_table(): jnp.einsum('kr,nrx->nkx', table, block, preferred_element_type=jnp.float32)  11.1 us
    dot_general x1, matrix products, density_terms(): jnp.einsum('aknm,bkmn->abk', left_real, prod_imag, precision=lax.Precisio...  7.35 us
    all_to_all x1, waiting for transfers between devices, per_device(): lax.all_to_all(imag_k, 'op', split_axis=1, concat_axis=0, tiled=True)  7.15 us
    dot_general x1, matrix products, density_terms(): jnp.einsum('aknm,bkmn->abk', left_imag, prod_real, precision=lax.Precisio...  6.79 us
    unnamed x2, other arithmetic  6.14 us
  transfers between devices with their start and end apart: 3, of which 3 were waited for; matrix products, arithmetic and copies ran while one was open for 9% of the time, Pallas kernels for 0%

profile of v1, /device:TPU:0, one launch (start us, length us, event | category | flops | bytes accessed | tf_op | source)
XLA Modules:
  0.0 180.2 jit_solution(12710832793720054370)
XLA Ops:
  7.9 13.8 %all-gather = s32[4,8,3]{1,2,0:T(4,128)S(1)} all-gather(s32[1,8,3]{1,2,0:T(4,128)} %bitcast.177), channel_id=1, replica_groups=mesh['ka'=4,'op'=4,'row'=2] {'op'}, dimensions={0}, use_global_device_ids=true | all-gather | bytes 480 | tf_op jit(solution)/shard_map/all_gather | solution.py:77
  23.3 35.9 %all-gather.3.cloned.1.call-done = bf16[1,256,12800]{2,1,0:T(8,128)(2,1)} async-done(((bf16[1,32,12800]{2,1,0:T(8,128)(2,1)}), bf16[1,256,12800]{2,1,0:T(8,128)(2,1)}) %all-gather.3.cloned.1.call-update) | async-done | bytes 6553616 | tf_op jit(solution)/shard_map/all_gather | solution.py:82
  59.1 2.8 %fusion.26 = f32[32,6400]{1,0:T(8,128)S(1)} fusion(bf16[1,256,12800]{2,1,0:T(8,128)(2,1)} %all-gather.3.cloned.1.call-done, f32[256]{0:T(256)S(1)} %convert_divide_fusion, s32[256]{0:T(256)S(1)} %bitcast.168, s32[32]{0:T(128)S(1)} %get-tuple-element.69, s32[256]{0:T(256)S(1)} %bitcast.172, s32[32]{0:T(128)S(1)} %get-tuple-element.70, s32[256]{0:T(256)S(1)} %bitcast.164, ...), kind=kOutput, calls=%fused_computation.35 | convolution fusion | flops 105021440 | bytes 4100480 | tf_op jit(solution)/shard_map/kr,nrx->nkx/dot_general | solution.py:27
  61.9 2.8 %fusion.25 = bf16[1,32,6400]{2,1,0:T(8,128)(2,1)S(1)} fusion(f32[32,6400]{1,0:T(8,128)S(1)} %fusion.26, bf16[1,256,12800]{2,1,0:T(8,128)(2,1)} %all-gather.3.cloned.1.call-done, f32[256]{0:T(256)S(1)} %convert_divide_fusion, s32[256]{0:T(256)S(1)} %bitcast.169, s32[32]{0:T(128)S(1)} %get-tuple-element.69, s32[256]{0:T(256)S(1)} %bitcast.173, ...), kind=kOutput, calls=%fused_computation.32 | convolution fusion | flops 105431040 | bytes 4510080 | tf_op jit(solution)/shard_map/kr,nrx->nkx/dot_general | solution.py:27
  65.8 3.1 %reduce.10 = bf16[32,6400]{1,0:T(8,128)(2,1)S(1)} reduce(bf16[32,1,6400]{2,1,0:T(2,128)(2,1)S(1)} %bitcast.162, bf16[]{:T(256)} %broadcast.118), dimensions={1}, to_apply=%bitcast.125.reduce_sub_computation | reduce | bytes 819202
  69.8 4.6 %all-to-all-start = ((bf16[4,2,25600]{2,1,0:T(2,128)(2,1)}), bf16[4,2,25600]{2,1,0:T(2,128)(2,1)S(1)}, u32[]{:S(2)}, u32[]{:S(2)}) async-start(bf16[4,2,25600]{2,1,0:T(2,128)(2,1)} %reshape.142), calls=%async_computation | async-start | bytes 819200 | tf_op jit(solution)/shard_map/all_to_all | solution.py:87
  74.4 2.8 %fusion.27 = f32[32,6400]{1,0:T(8,128)S(1)} fusion(bf16[1,256,12800]{2,1,0:T(8,128)(2,1)} %all-gather.3.cloned.1.call-done, f32[256]{0:T(256)S(1)} %convert_divide_fusion, s32[256]{0:T(256)S(1)} %bitcast.170, s32[32]{0:T(128)S(1)} %get-tuple-element.69, s32[256]{0:T(256)S(1)} %bitcast.174, s32[32]{0:T(128)S(1)} %get-tuple-element.70, s32[256]{0:T(256)S(1)} %bitcast.166, ...), kind=kOutput, calls=%fused_computation.36 | convolution fusion | flops 105021440 | bytes 4100480 | tf_op jit(solution)/shard_map/kr,nrx->nkx/dot_general | solution.py:27
  77.2 2.8 %fusion.24 = bf16[1,32,6400]{2,1,0:T(8,128)(2,1)S(1)} fusion(f32[32,6400]{1,0:T(8,128)S(1)} %fusion.27, bf16[1,256,12800]{2,1,0:T(8,128)(2,1)} %all-gather.3.cloned.1.call-done, f32[256]{0:T(256)S(1)} %convert_divide_fusion, s32[256]{0:T(256)S(1)} %bitcast.171, s32[32]{0:T(128)S(1)} %get-tuple-element.69, s32[256]{0:T(256)S(1)} %bitcast.175, ...), kind=kOutput, calls=%fused_computation.31 | convolution fusion | flops 105431040 | bytes 4510080 | tf_op jit(solution)/shard_map/kr,nrx->nkx/dot_general | solution.py:27
  80.6 3.1 %reduce.11 = bf16[32,6400]{1,0:T(8,128)(2,1)S(1)} reduce(bf16[32,1,6400]{2,1,0:T(2,128)(2,1)S(1)} %bitcast.163, bf16[]{:T(256)} %broadcast.118), dimensions={1}, to_apply=%bitcast.124.reduce_sub_computation | reduce | bytes 819202
  84.6 2.3 %all-to-all-done = bf16[4,2,25600]{2,1,0:T(2,128)(2,1)S(1)} async-done(((bf16[4,2,25600]{2,1,0:T(2,128)(2,1)}), bf16[4,2,25600]{2,1,0:T(2,128)(2,1)S(1)}, u32[]{:S(2)}, u32[]{:S(2)}) %all-to-all-start) | async-done | bytes 409632 | tf_op jit(solution)/shard_map/all_to_all | solution.py:87
  86.8 3.6 %all-to-all-start.1 = ((bf16[4,2,25600]{2,1,0:T(2,128)(2,1)}), bf16[4,2,25600]{2,1,0:T(2,128)(2,1)S(1)}, u32[]{:S(2)}, u32[]{:S(2)}) async-start(bf16[4,2,25600]{2,1,0:T(2,128)(2,1)} %reshape.144), calls=%async_computation.1 | async-start | bytes 819200 | tf_op jit(solution)/shard_map/all_to_all | solution.py:88
  91.4 2.3 %bitcast_reduce_fusion.1 = bf16[32,6400]{1,0:T(8,128)(2,1)S(1)} fusion(bf16[32,1,6400]{2,1,0:T(2,128)(2,1)S(1)} %reshape.143), kind=kLoop, calls=%fused_computation.108 | loop fusion | bytes 819200 | tf_op jit(solution)/shard_map/all_to_all | solution.py:87
  94.7 7.1 %all-to-all-done.1 = bf16[4,2,25600]{2,1,0:T(2,128)(2,1)S(1)} async-done(((bf16[4,2,25600]{2,1,0:T(2,128)(2,1)}), bf16[4,2,25600]{2,1,0:T(2,128)(2,1)S(1)}, u32[]{:S(2)}, u32[]{:S(2)}) %all-to-all-start.1) | async-done | bytes 409632 | tf_op jit(solution)/shard_map/all_to_all | solution.py:88
  102.2 2.3 %bitcast_reduce_fusion = bf16[32,6400]{1,0:T(8,128)(2,1)S(1)} fusion(bf16[32,1,6400]{2,1,0:T(2,128)(2,1)S(1)} %reshape.145), kind=kLoop, calls=%fused_computation.107 | loop fusion | bytes 819200 | tf_op jit(solution)/shard_map/all_to_all | solution.py:88
  105.6 7.9 %while.12 = (s32[]{:T(128)}, bf16[4,8,80,80]{2,3,1,0:T(8,128)(2,1)S(1)}, bf16[4,8,80,80]{2,3,1,0:T(8,128)(2,1)S(1)}, bf16[4,8,80,80]{3,2,1,0:T(8,128)(2,1)S(1)},...) while((s32[]{:T(128)}, ...), condition=%wide.region_1.2_spmd, body=%wide.region_0.1_spmd.sunk | while | flops 65945600 | bytes 5038189 | solution.py:116
  115.7 3.7 %gather_fusion = bf16[80,8]{1,0:T(8,128)(2,1)S(1)} fusion(bf16[8,80,80]{0,2,1:T(8,128)(2,1)} %copy.74, s32[80]{0:T(128)S(1)} %or_bitcast_fusion), kind=kCustom, calls=%fused_computation | custom fusion | bytes 3200 | tf_op jit(solution)/shard_map/jit(diagonal)/gather | solution.py:49
  121.9 2.2 %fusion.28 = f32[3,8,80,80]{2,3,0,1:T(8,128)} fusion(f32[8,3,80,80]{3,2,1,0:T(8,128)S(1)} %fusion.46, bf16[4,8,80,80]{3,2,1,0:T(8,128)(2,1)} %copy.73, bf16[4,8,80,80]{2,3,1,0:T(8,128)(2,1)S(1)} %get-tuple-element.40), kind=kOutput, calls=%fused_computation.38 | convolution fusion | flops 24729600 | bytes 1802240 | tf_op jit(solution)/shard_map/knm,bkml->bknl/dot_general | solution.py:54
  124.1 2.4 %copy.78 = f32[3,8,80,80]{3,0,2,1:T(4,128)} copy(f32[3,8,80,80]{2,3,0,1:T(8,128)} %fusion.28) | data formatting | bytes 1228800 | tf_op jit(solution)/shard_map/sub | solution.py:56
  127.7 2.1 %fusion.29 = f32[3,8,80,80]{2,3,0,1:T(8,128)} fusion(f32[8,3,80,80]{3,2,1,0:T(8,128)S(1)} %fusion.48, bf16[4,8,80,80]{3,2,1,0:T(8,128)(2,1)} %copy.73, bf16[4,8,80,80]{2,3,1,0:T(8,128)(2,1)S(1)} %get-tuple-element.41), kind=kOutput, calls=%fused_computation.40 | convolution fusion | flops 24729600 | bytes 1802240 | tf_op jit(solution)/shard_map/knm,bkml->bknl/dot_general | solution.py:54
  129.9 2.4 %copy.76 = f32[3,8,80,80]{3,0,2,1:T(4,128)} copy(f32[3,8,80,80]{2,3,0,1:T(8,128)} %fusion.29) | data formatting | bytes 1228800 | tf_op jit(solution)/shard_map/add | solution.py:57
  132.3 7.4 %fusion.34 = f32[8,3,3]{2,1,0:T(4,128)S(1)} fusion(f32[3,8,80,80]{3,0,2,1:T(4,128)} %copy.76, f32[3,8,80,80]{2,3,0,1:T(8,128)S(1)} %get-tuple-element.62), kind=kOutput, calls=%fused_computation.45 | convolution fusion | flops 5529600 | bytes 1229088 | tf_op jit(solution)/shard_map/aknm,bkmn->abk/dot_general | solution.py:61
  139.7 6.8 %fusion.43 = f32[3,3,8]{0,1,2:T(4,128)S(1)} fusion(f32[8,3,3]{2,1,0:T(4,128)S(1)} %fusion.34, f32[3,8,80,80]{3,0,2,1:T(4,128)} %copy.78, f32[3,8,80,80]{2,3,0,1:T(8,128)S(1)} %copy-done), kind=kOutput, calls=%fused_computation.48 | convolution fusion | flops 5529672 | bytes 1229376 | tf_op jit(solution)/shard_map/aknm,bkmn->abk/dot_general | solution.py:63
  147.4 19.5 %psum.14 = f32[3]{0:T(128)S(1)} all-reduce(f32[3]{0:T(128)S(1)} %get-tuple-element.59), channel_id=1, replica_groups=mesh['ka'=4,'op'=4,'row'=2] {'op','row'}, use_global_device_ids=true, to_apply=%region_3.4 | all-reduce | flops 3 | bytes 24 | tf_op jit(solution)/shard_map/psum | solution.py:120
  166.8 6.0 %psum.15 = f32[3]{0:T(128)S(1)} all-reduce(f32[3]{0:T(128)S(1)} %psum.14), channel_id=1, replica_groups=mesh['ka'=4,'op'=4,'row'=2] {'ka'}, use_global_device_ids=true, to_apply=%region_4.5 | all-reduce | flops 3 | bytes 24 | tf_op jit(solution)/shard_map/psum | solution.py:120
  (73 shorter events, 24.2 us)
Async XLA Ops:
  7.2 51.9 %all-gather.3.cloned.1.call-start = ((), (), s32[]{:S(2)}) async-start(), calls=%async_computation.2 | async-start | bytes 7372800 | tf_op jit(solution)/shard_map/all_gather | solution.py:82
  69.8 17.0 %all-to-all-start = ((bf16[4,2,25600]{2,1,0:T(2,128)(2,1)}), bf16[4,2,25600]{2,1,0:T(2,128)(2,1)S(1)}, u32[]{:S(2)}, u32[]{:S(2)}) async-start(bf16[4,2,25600]{2,1,0:T(2,128)(2,1)} %reshape.142), calls=%async_computation | async-start | bytes 819200 | tf_op jit(solution)/shard_map/all_to_all | solution.py:87
  77.2 13.4 %copy-start.2 = (bf16[8,12800]{1,0:T(8,128)(2,1)S(1)}, bf16[8,12800]{1,0:T(8,128)(2,1)}, u32[]{:S(2)}) copy-start(bf16[8,12800]{1,0:T(8,128)(2,1)} %param.11) | copy-start | bytes 614404
  86.8 15.0 %all-to-all-start.1 = ((bf16[4,2,25600]{2,1,0:T(2,128)(2,1)}), bf16[4,2,25600]{2,1,0:T(2,128)(2,1)S(1)}, u32[]{:S(2)}, u32[]{:S(2)}) async-start(bf16[4,2,25600]{2,1,0:T(2,128)(2,1)} %reshape.144), calls=%async_computation.1 | async-start | bytes 819200 | tf_op jit(solution)/shard_map/all_to_all | solution.py:88
  113.8 5.7 %copy-start.1 = (bf16[4,8,80,80]{3,2,1,0:T(8,128)(2,1)}, bf16[4,8,80,80]{3,2,1,0:T(8,128)(2,1)S(1)}, u32[]{:S(2)}) copy-start(bf16[4,8,80,80]{3,2,1,0:T(8,128)(2,1)S(1)} %copy.71) | copy-start | bytes 1228804
  129.9 9.8 %copy-start = (f32[3,8,80,80]{2,3,0,1:T(8,128)S(1)}, f32[3,8,80,80]{2,3,0,1:T(8,128)}, u32[]{:S(2)}) copy-start(f32[3,8,80,80]{2,3,0,1:T(8,128)} %get-tuple-element.61) | copy-start | bytes 1843204
Sparse Core Ops, SparseCore 0:
  9.9 49.2 all-gather.2
